TPU v7x, 256 devices: a whole 4x4x8 slice. The times are simulated.
256 devices in a mesh: px: 4 (over z_hi), py: 8 (over z_lo, y), sa: 8 (over x, core).
Axes of the slice: x: 4, y: 4, z: 8 (z_hi: 4, z_lo: 2; z = z_hi * 2 + z_lo), core: 2. Of those that a mesh axis runs over, the one named last changes fastest.
Arguments:
- real_coeffs: float32 [8, 256, 256, 256], P('sa', 'px', 'py'), may hold values from -6 to 6
- imaginary_coeffs: float32 [8, 256, 256, 256], P('sa', 'px', 'py'), may hold values from -6 to 6
Outputs:
- modulus: float32 [8, 256, 256, 256], P(None, ('px', 'py'), 'sa')
All inputs are finite; a program needn't handle non-finite values.
Results may differ from a plain program's by a relative error of at most 0.00007.
Values sent between devices are 32-bit elements; how exact they have to be, the bound alone decides.
A program may use at most 64 MiB of HBM per device.

v0:
```python
from functools import partial
import math

import jax
import jax.numpy as jnp
from jax import lax
from jax.sharding import PartitionSpec as P

corr_length = 1.0
log_spread = 0.5


def matern(squared, length):
    return 1.0 / (1.0 + (2.0 * math.pi * corr_length / length) ** 2 * squared)


def matern_scale(length):
    middle = length // 2
    square_counts = {}
    for position in range(length):
        square_value = ((position + middle) % length - middle) ** 2
        square_counts[square_value] = square_counts.get(square_value, 0) + 1
    plane_counts = {}
    for first_square, first_count in square_counts.items():
        for second_square, second_count in square_counts.items():
            plane_sum = first_square + second_square
            plane_counts[plane_sum] = plane_counts.get(plane_sum, 0) + first_count * second_count
    running = 0.0
    for first_square, first_count in square_counts.items():
        for plane_sum, plane_count in plane_counts.items():
            running = (
                running + first_count * plane_count * matern(first_square + plane_sum, length) ** 2
            )
    return 1.0 / math.sqrt(running)


def signed(positions, length):
    return (positions + length // 2) % length - length // 2


def phase_tables(length, waves):
    positions = lax.iota(jnp.int32, length)
    phases = positions[:, None] * waves[None, :] % length
    angles = phases.astype(jnp.float32) * (2.0 * math.pi / length)
    return (jnp.cos(angles), jnp.sin(angles))


def transform(form, tables, pieces):
    cos_table, sin_table = tables
    real_in, imag_in = pieces
    product = partial(jnp.einsum, form, precision=lax.Precision.HIGHEST)
    real_out = product(cos_table, real_in) - product(sin_table, imag_in)
    imag_out = product(sin_table, real_in) + product(cos_table, imag_in)
    return (real_out, imag_out)


def finish(pieces, z_tables):
    cos_table, sin_table = z_tables
    product = partial(jnp.einsum, "zk,skxy->sxyz", precision=lax.Precision.HIGHEST)
    log_field = product(cos_table, pieces[0]) - product(sin_table, pieces[1])
    return jnp.exp(log_spread * log_field)


def z_phase_tables(length, rows_z, across_x, across_y):
    quarter = rows_z // across_x
    places = lax.iota(jnp.int32, length)
    sender = places // quarter
    z_waves = sender % across_y * rows_z + sender // across_y * quarter + places % quarter
    return phase_tables(length, z_waves)


def local(real_coeffs, imaginary_coeffs):
    length = real_coeffs.shape[3]
    rows_y = real_coeffs.shape[1]
    rows_z = real_coeffs.shape[2]
    across_x = lax.axis_size("px")
    across_y = lax.axis_size("py")
    freq_x = signed(lax.iota(jnp.int32, length), length).astype(jnp.float32)
    freq_y = signed(lax.iota(jnp.int32, rows_y) + lax.axis_index("px") * rows_y, length).astype(
        jnp.float32
    )
    freq_z = signed(lax.iota(jnp.int32, rows_z) + lax.axis_index("py") * rows_z, length).astype(
        jnp.float32
    )
    squared = freq_x[None, None, :] ** 2 + freq_y[:, None, None] ** 2 + freq_z[None, :, None] ** 2
    weight = matern(squared, length) * matern_scale(length)
    tables = phase_tables(length, lax.iota(jnp.int32, length))
    x_real, x_imag = transform(
        "xk,sabk->sabx", tables, (real_coeffs * weight, imaginary_coeffs * weight)
    )
    y_real, y_imag = transform(
        "yk,skqx->sqxy",
        tables,
        (
            lax.all_to_all(x_real, "px", split_axis=2, concat_axis=1, tiled=True),
            lax.all_to_all(x_imag, "px", split_axis=2, concat_axis=1, tiled=True),
        ),
    )
    z_tables = z_phase_tables(length, rows_z, across_x, across_y)
    local_field = finish(
        (
            lax.all_to_all(y_real, ("px", "py"), split_axis=2, concat_axis=1, tiled=True),
            lax.all_to_all(y_imag, ("px", "py"), split_axis=2, concat_axis=1, tiled=True),
        ),
        z_tables,
    )
    return lax.all_to_all(local_field, "sa", split_axis=2, concat_axis=0, tiled=True)


def solution(mesh):
    placed = (P("sa", "px", "py", None), P("sa", "px", "py", None))
    return jax.shard_map(
        local,
        mesh=mesh,
        in_specs=placed,
        out_specs=P(None, ("px", "py"), "sa", None),
        check_vma=False,
    )
```

profile of v0, /device:TPU:1, one launch (start us, length us, event | category | flops | bytes accessed | tf_op | source)
XLA Modules:
  0.0 295.5 jit_solution(10025072752009620852)
XLA Ops:
  0.1 4.9 %fusion = f32[64,32,256]{2,1,0:T(8,128)S(1)} fusion(f32[1,64,32,256]{3,2,1,0:T(8,128)} %param.3, f32[32]{0:T(128)S(1)} %fusion.72, f32[64,256]{1,0:T(8,128)S(1)} %broadcast_add_fusion), kind=kOutput, calls=%fused_computation | convolution fusion | flops 1614675968 | bytes 4259968 | tf_op jit(solution)/shard_map/xk,sabk->sabx/dot_general | solution.py:53
  5.0 3.3 %add_bitcast_fusion.1 = f32[1,64,32,256]{3,2,1,0:T(8,128)S(1)} fusion(f32[64,32,256]{2,1,0:T(8,128)S(1)} %fusion, f32[1,64,32,256]{3,2,1,0:T(8,128)S(1)} %copy-done.1, f32[32]{0:T(128)S(1)} %fusion.72, f32[64,256]{1,0:T(8,128)S(1)} %broadcast_add_fusion), kind=kOutput, calls=%fused_computation.20 | convolution fusion | flops 1615200256 | bytes 6357120 | tf_op jit(solution)/shard_map/xk,sabk->sabx/dot_general | solution.py:53
  8.3 2.6 copy.35
  10.8 9.2 %all-to-all-start.1 = ((f32[1,64,32,256]{3,1,0,2:T(8,128)}), f32[1,64,32,256]{3,1,0,2:T(8,128)S(1)}, u32[]{:S(2)}, u32[]{:S(2)}) async-start(f32[1,64,32,256]{3,1,0,2:T(8,128)} %copy.35), calls=%async_computation.1 | async-start | bytes 4194304 | tf_op jit(solution)/shard_map/all_to_all | solution.py:96
  20.1 5.0 %fusion.2 = f32[64,32,256]{2,1,0:T(8,128)S(1)} fusion(f32[1,64,32,256]{3,2,1,0:T(8,128)} %param.3, f32[32]{0:T(128)S(1)} %fusion.72, f32[64,256]{1,0:T(8,128)S(1)} %broadcast_add_fusion), kind=kOutput, calls=%fused_computation.2 | convolution fusion | flops 1614675968 | bytes 4259968 | tf_op jit(solution)/shard_map/xk,sabk->sabx/dot_general | solution.py:52
  25.1 3.2 %subtract_bitcast_fusion.1 = f32[1,64,32,256]{3,2,1,0:T(8,128)S(1)} fusion(f32[64,32,256]{2,1,0:T(8,128)S(1)} %fusion.2, f32[1,64,32,256]{3,2,1,0:T(8,128)S(1)} %copy-done.2, f32[32]{0:T(128)S(1)} %fusion.72, f32[64,256]{1,0:T(8,128)S(1)} %broadcast_add_fusion), kind=kOutput, calls=%fused_computation.21 | convolution fusion | flops 1615200256 | bytes 6357120 | tf_op jit(solution)/shard_map/xk,sabk->sabx/dot_general | solution.py:52
  28.3 2.5 copy.31
  30.8 34.7 %all-to-all-done.1 = f32[1,64,32,256]{3,1,0,2:T(8,128)S(1)} async-done(((f32[1,64,32,256]{3,1,0,2:T(8,128)}), f32[1,64,32,256]{3,1,0,2:T(8,128)S(1)}, u32[]{:S(2)}, u32[]{:S(2)}) %all-to-all-start.1) | async-done | bytes 2097184 | tf_op jit(solution)/shard_map/all_to_all | solution.py:96
  65.5 6.7 %all-to-all-start = ((f32[1,64,32,256]{3,1,0,2:T(8,128)}), f32[1,64,32,256]{3,1,0,2:T(8,128)}, u32[]{:S(2)}, u32[]{:S(2)}) async-start(f32[1,64,32,256]{3,1,0,2:T(8,128)} %copy.31), calls=%async_computation | async-start | bytes 4194304 | tf_op jit(solution)/shard_map/all_to_all | solution.py:95
  76.9 23.7 %all-to-all-done = f32[1,64,32,256]{3,1,0,2:T(8,128)} async-done(((f32[1,64,32,256]{3,1,0,2:T(8,128)}), f32[1,64,32,256]{3,1,0,2:T(8,128)}, u32[]{:S(2)}, u32[]{:S(2)}) %all-to-all-start) | async-done | bytes 2097184 | tf_op jit(solution)/shard_map/all_to_all | solution.py:95
  100.6 2.8 copy.66
  104.9 2.9 copy.34
  107.8 4.4 %fusion.35 = f32[8,256,256]{2,1,0:T(8,128)S(1)} fusion(f32[256,8,256]{0,2,1:T(8,128)} %copy.34), kind=kOutput, calls=%fused_computation.46 | convolution fusion | flops 1611530240 | bytes 4194304 | tf_op jit(solution)/shard_map/yk,skqx->sqxy/dot_general | solution.py:52
  112.2 2.9 subtract_bitcast_fusion
  115.2 2.5 copy.39
  117.7 26.9 %all-to-all-start.2 = ((f32[1,8,256,256]{3,1,0,2:T(8,128)}), f32[1,8,256,256]{3,1,0,2:T(8,128)}, u32[]{:S(2)}, u32[]{:S(2)}) async-start(f32[1,8,256,256]{3,1,0,2:T(8,128)} %copy.39), calls=%async_computation.2 | async-start | bytes 4194304 | tf_op jit(solution)/shard_map/all_to_all | solution.py:102
  144.7 4.4 %fusion.28 = f32[8,256,256]{2,1,0:T(8,128)S(1)} fusion(f32[256,8,256]{0,2,1:T(8,128)} %copy.34), kind=kOutput, calls=%fused_computation.39 | convolution fusion | flops 1611530240 | bytes 4194304 | tf_op jit(solution)/shard_map/yk,skqx->sqxy/dot_general | solution.py:53
  149.1 2.9 add_bitcast_fusion
  154.5 36.6 %all-to-all-done.2 = f32[1,8,256,256]{3,1,0,2:T(8,128)} async-done(((f32[1,8,256,256]{3,1,0,2:T(8,128)}), f32[1,8,256,256]{3,1,0,2:T(8,128)}, u32[]{:S(2)}, u32[]{:S(2)}) %all-to-all-start.2) | async-done | bytes 2097184 | tf_op jit(solution)/shard_map/all_to_all | solution.py:102
  191.1 7.1 %all-to-all-start.3 = ((f32[1,8,256,256]{3,1,0,2:T(8,128)}), f32[1,8,256,256]{3,1,0,2:T(8,128)S(1)}, u32[]{:S(2)}, u32[]{:S(2)}) async-start(f32[1,8,256,256]{3,1,0,2:T(8,128)} %copy.45), calls=%async_computation.3 | async-start | bytes 4194304 | tf_op jit(solution)/shard_map/all_to_all | solution.py:103
  202.1 41.9 %all-to-all-done.3 = f32[1,8,256,256]{3,1,0,2:T(8,128)S(1)} async-done(((f32[1,8,256,256]{3,1,0,2:T(8,128)}), f32[1,8,256,256]{3,1,0,2:T(8,128)S(1)}, u32[]{:S(2)}, u32[]{:S(2)}) %all-to-all-start.3) | async-done | bytes 2097184 | tf_op jit(solution)/shard_map/all_to_all | solution.py:103
  244.9 4.7 %fusion.8 = f32[8,256,256]{2,1,0:T(8,128)S(1)} fusion(f32[256,8,256]{2,1,0:T(8,128)S(1)} %bitcast.82, s32[256]{0:T(256)S(1)} %fusion.60), kind=kOutput, calls=%fused_computation.9 | convolution fusion | flops 1611530240 | bytes 4195328 | tf_op jit(solution)/shard_map/zk,skxy->sxyz/dot_general | solution.py:60
  249.7 4.8 %exponential_bitcast_fusion = f32[1,8,256,256]{3,2,1,0:T(8,128)S(1)} fusion(f32[8,256,256]{2,1,0:T(8,128)S(1)} %fusion.8, f32[256,8,256]{2,1,0:T(8,128)S(1)} %bitcast.83, s32[256]{0:T(256)S(1)} %fusion.60), kind=kOutput, calls=%fused_computation.17 | convolution fusion | flops 1612578816 | bytes 6292480 | tf_op jit(solution)/shard_map/zk,skxy->sxyz/dot_general | solution.py:60
  255.7 37.6 %all_to_all.78 = f32[1,8,256,256]{3,1,0,2:T(8,128)S(1)} all-to-all(f32[1,8,256,256]{3,1,0,2:T(8,128)S(1)} %copy.49), channel_id=1, replica_groups=mesh['px'=4,'py'=8,'sa'=8] {'sa'}, dimensions={2} | all-to-all | bytes 4194304 | tf_op jit(solution)/shard_map/all_to_all | solution.py:107
  (22 shorter events, 16.7 us)
Async XLA Ops:
  0.1 4.9 %copy-start.1 = (f32[1,64,32,256]{3,2,1,0:T(8,128)S(1)}, f32[1,64,32,256]{3,2,1,0:T(8,128)}, u32[]{:S(2)}) copy-start(f32[1,64,32,256]{3,2,1,0:T(8,128)} %param.2) | copy-start | bytes 6291460
  10.8 54.7 %all-to-all-start.1 = ((f32[1,64,32,256]{3,1,0,2:T(8,128)}), f32[1,64,32,256]{3,1,0,2:T(8,128)S(1)}, u32[]{:S(2)}, u32[]{:S(2)}) async-start(f32[1,64,32,256]{3,1,0,2:T(8,128)} %copy.35), calls=%async_computation.1 | async-start | bytes 4194304 | tf_op jit(solution)/shard_map/all_to_all | solution.py:96
  20.0 5.0 %copy-start.2 = (f32[1,64,32,256]{3,2,1,0:T(8,128)S(1)}, f32[1,64,32,256]{3,2,1,0:T(8,128)}, u32[]{:S(2)}) copy-start(f32[1,64,32,256]{3,2,1,0:T(8,128)} %param.2) | copy-start | bytes 6291460
  65.5 35.1 %all-to-all-start = ((f32[1,64,32,256]{3,1,0,2:T(8,128)}), f32[1,64,32,256]{3,1,0,2:T(8,128)}, u32[]{:S(2)}, u32[]{:S(2)}) async-start(f32[1,64,32,256]{3,1,0,2:T(8,128)} %copy.31), calls=%async_computation | async-start | bytes 4194304 | tf_op jit(solution)/shard_map/all_to_all | solution.py:95
  117.7 73.4 %all-to-all-start.2 = ((f32[1,8,256,256]{3,1,0,2:T(8,128)}), f32[1,8,256,256]{3,1,0,2:T(8,128)}, u32[]{:S(2)}, u32[]{:S(2)}) async-start(f32[1,8,256,256]{3,1,0,2:T(8,128)} %copy.39), calls=%async_computation.2 | async-start | bytes 4194304 | tf_op jit(solution)/shard_map/all_to_all | solution.py:102
  191.1 52.8 %all-to-all-start.3 = ((f32[1,8,256,256]{3,1,0,2:T(8,128)}), f32[1,8,256,256]{3,1,0,2:T(8,128)S(1)}, u32[]{:S(2)}, u32[]{:S(2)}) async-start(f32[1,8,256,256]{3,1,0,2:T(8,128)} %copy.45), calls=%async_computation.3 | async-start | bytes 4194304 | tf_op jit(solution)/shard_map/all_to_all | solution.py:103
  244.9 4.8 %copy-start = (f32[1,32,8,8,256]{4,3,2,1,0:T(8,128)S(1)}, f32[1,32,8,8,256]{4,3,2,1,0:T(8,128)}, u32[]{:S(2)}) copy-start(f32[1,32,8,8,256]{4,3,2,1,0:T(8,128)} %copy.41) | copy-start | bytes 6291460
where the time goes:
time: 301 us; the launch traced here: 295 us
  waiting for transfers between devices  137 us (46%)
  starting transfers between devices  49.9 us (17%)
  matrix products  40.5 us (13%)
  blocking collectives  37.6 us (12%)
  local copies, waits for them, and re-layouts  30 us (10%)
    all_to_all x1, waiting for transfers between devices, local(): lax.all_to_all(y_imag, ('px', 'py'), split_axis=2, concat_axis=1, tiled=T...  41.9 us
    all_to_all x1, blocking collectives, local(): lax.all_to_all(local_field, 'sa', split_axis=2, concat_axis=0, tiled=True)  37.6 us
    all_to_all x1, waiting for transfers between devices, local(): lax.all_to_all(y_real, ('px', 'py'), split_axis=2, concat_axis=1, tiled=T...  36.6 us
    all_to_all x1, waiting for transfers between devices, local(): lax.all_to_all(x_imag, 'px', split_axis=2, concat_axis=1, tiled=True)  34.7 us
    all_to_all x1, starting transfers between devices, local(): lax.all_to_all(y_real, ('px', 'py'), split_axis=2, concat_axis=1, tiled=T...  26.9 us
    all_to_all x1, waiting for transfers between devices, local(): lax.all_to_all(x_real, 'px', split_axis=2, concat_axis=1, tiled=True)  23.7 us
    dot_general x4, matrix products, transform(): real_out = product(cos_table, real_in) - product(sin_table, imag_in)  15.5 us
    dot_general x4, matrix products, transform(): imag_out = product(sin_table, real_in) + product(cos_table, imag_in)  15.4 us
  transfers between devices with their start and end apart: 4, of which 4 were waited for; matrix products, arithmetic and copies ran while one was open for 10% of the time, Pallas kernels for 0%

commit v1 on v0

v1 whole, which is shorter than its diff:
```python
import math

import jax
import jax.numpy as jnp
import numpy as np
from jax import lax
from jax.experimental import pallas as pl
from jax.experimental.pallas import tpu as pltpu
from jax.sharding import PartitionSpec as P

MESH = pl.DeviceIdType.MESH
corr_length = 1.0
log_spread = 0.5

N = 256
GROUP = 32
CHUNKS = 8
PITCH = 40


def matern(squared, length):
    return 1.0 / (1.0 + (2.0 * math.pi * corr_length / length) ** 2 * squared)


def matern_scale(length):
    middle = length // 2
    square_counts = {}
    for position in range(length):
        square_value = ((position + middle) % length - middle) ** 2
        square_counts[square_value] = square_counts.get(square_value, 0) + 1
    plane_counts = {}
    for first_square, first_count in square_counts.items():
        for second_square, second_count in square_counts.items():
            plane_sum = first_square + second_square
            plane_counts[plane_sum] = plane_counts.get(plane_sum, 0) + first_count * second_count
    running = 0.0
    for first_square, first_count in square_counts.items():
        for plane_sum, plane_count in plane_counts.items():
            running = (
                running + first_count * plane_count * matern(first_square + plane_sum, length) ** 2
            )
    return 1.0 / math.sqrt(running)


def halves(table):
    high = table.astype(np.float32).astype(jnp.bfloat16)
    low = (table - high.astype(np.float64)).astype(np.float32).astype(jnp.bfloat16)
    return high, low


def phases(rows, columns):
    angles = (np.asarray(rows)[:, None] * np.asarray(columns)[None, :] % N) * (2.0 * np.pi / N)
    return np.cos(angles), np.sin(angles)


def x_table():
    pieces = []
    for j in range(CHUNKS):
        cos, sin = phases(np.arange(GROUP) * CHUNKS + j, np.arange(N))
        pieces.append(np.block([[cos, -sin], [sin, cos]]))
    high, low = halves(np.stack(pieces))
    return np.concatenate([high, low], axis=1)


def z_table():
    odd, owner, pair = np.meshgrid(np.arange(2), np.arange(8), np.arange(16), indexing="ij")
    waves = (owner * 32 + pair * 2 + odd).reshape(-1)
    cos, sin = phases(np.arange(N), waves)
    high, low = halves(np.block([[cos, -sin], [sin, cos]]))
    return np.concatenate([high, low], axis=0)


def y_table():
    cos, sin = phases(np.arange(N), np.arange(N))
    high, low = halves(np.concatenate([cos, -sin], axis=1))
    return np.concatenate([high, low], axis=0)


def split(value):
    high = value.astype(jnp.bfloat16)
    low = (value - high.astype(jnp.float32)).astype(jnp.bfloat16)
    return high, low


def dot(left, right, transposed):
    return lax.dot_general(
        left,
        right,
        (((1,), (1 if transposed else 0,)), ((), ())),
        preferred_element_type=jnp.float32,
    )


def signed(positions):
    return ((positions + N // 2) % N - N // 2).astype(jnp.float32)


def kernel(
    re_hbm, im_hbm, tx_hbm, tz_hbm, ty_hbm, out_ref,
    xbuf, dhigh, dlow, gbuf, rbuf, obuf, tx, tz, ty, whigh, wlow, bhigh, blow,
    in_sem, table_sem, send_sem, recv_sem, out_send_sem, out_recv_sem,
):
    px, py, sa = lax.axis_index("px"), lax.axis_index("py"), lax.axis_index("sa")
    me = px * 8 + py
    z, y = px * 2 + py // 4, py % 4

    def plane_peer(dz, dy):
        z2, y2 = (z + dz) % 8, (y + dy) % 4
        return z2 // 2, (z2 % 2) * 4 + y2

    order = (4, 3, -3, 2, -2, 1, -1, 0)
    offsets = [(dz, dy) for dz in order for dy in range(4) if (dz, dy) != (0, 0)]

    barrier = pltpu.get_barrier_semaphore()
    for dz, dy in offsets:
        p, q = plane_peer(dz, dy)
        pl.semaphore_signal(barrier, inc=1, device_id={"px": p, "py": q}, device_id_type=MESH)
    for step in range(1, 8):
        pl.semaphore_signal(
            barrier, inc=1, device_id={"sa": (sa + step) % 8}, device_id_type=MESH
        )

    table_copies = [
        pltpu.make_async_copy(tx_hbm, tx, table_sem.at[0]),
        pltpu.make_async_copy(tz_hbm, tz, table_sem.at[1]),
        pltpu.make_async_copy(ty_hbm, ty, table_sem.at[2]),
    ]
    in_copies = []
    for block in range(4):
        group = []
        for part, source in enumerate((re_hbm, im_hbm)):
            for half in range(2):
                copy = pltpu.make_async_copy(
                    source.at[0, :, pl.ds(block * 8, 8), pl.ds(half * 128, 128)],
                    xbuf.at[part * 2 + half, :, pl.ds(block * 8, 8), :],
                    in_sem.at[block, part * 2 + half],
                )
                copy.start()
                group.append(copy)
        in_copies.append(group)
        if block == 0:
            table_copies[0].start()
    table_copies[1].start()
    table_copies[2].start()

    scale = matern_scale(N)
    slope = (2.0 * math.pi * corr_length / N) ** 2
    fy = signed(lax.broadcasted_iota(jnp.int32, (64, 128), 0) + px * 64) ** 2
    lanes = lax.broadcasted_iota(jnp.int32, (64, 128), 1)
    flat = signed(lanes) ** 2 + fy, signed(lanes + 128) ** 2 + fy
    lines = xbuf.reshape(4, 64 * PITCH, 128)

    for block in range(4):
        for copy in in_copies[block]:
            copy.wait()

        def weigh(step, carry, block=block):
            k = block * 8 + step
            fz = signed(py * 32 + k) ** 2
            rows = pl.ds(pl.multiple_of(k * 64, 64), 64)
            for half in range(2):
                weight = (1.0 / (1.0 + slope * (flat[half] + fz))) * scale
                for part in range(2):
                    value = lines[part * 2 + half, pl.ds(k, 64, stride=PITCH), :] * weight
                    high, low = split(value)
                    columns = pl.ds(part * N + half * 128, 128)
                    dhigh[rows, columns] = high
                    dlow[rows, columns] = low
            return carry

        lax.fori_loop(0, 8, weigh, 0)
    table_copies[0].wait()

    pl.semaphore_wait(barrier, len(offsets) + 7)

    def message(j, d):
        return gbuf.at[pl.ds(pl.multiple_of((j * GROUP + d) * PITCH, 8), 32), :]

    def forward(j, carry):
        base = j * (GROUP * PITCH)
        for block in range(8):
            rows = pl.ds(block * 256, 256)
            both = dot(tx[j], dhigh[rows, :], True)
            piece = both[:64] + both[64:] + dot(tx[j, :64], dlow[rows, :], True)
            for part in range(2):
                for half in range(2):
                    at = base + part * 16 + block * 2 + half
                    gbuf[pl.ds(at, GROUP, stride=PITCH), :] = piece[
                        part * 32 : part * 32 + 32, half * 128 : half * 128 + 128
                    ]
        for dz, dy in offsets:
            p, q = plane_peer(dz, dy)
            pltpu.make_async_remote_copy(
                src_ref=message(j, p * 8 + q),
                dst_ref=rbuf.at[j, me],
                send_sem=send_sem.at[j],
                recv_sem=recv_sem.at[j],
                device_id={"px": p, "py": q},
                device_id_type=MESH,
            ).start()
        rbuf[j, me] = gbuf[pl.ds(pl.multiple_of((j * GROUP + me) * PITCH, 8), 32), :]
        return carry

    lax.fori_loop(0, CHUNKS, forward, 0)
    table_copies[1].wait()
    table_copies[2].wait()

    low_lanes = lax.broadcasted_iota(jnp.int32, (128, 128), 1) < 64

    def finish(j, carry):
        arrived = rbuf.at[j, pl.ds(0, GROUP - 1)]
        pltpu.make_async_copy(arrived, arrived, recv_sem.at[j]).wait()
        for part in range(2):
            for pair in range(2):
                first, second = (
                    rbuf[
                        j, pl.ds((pair * 2 + k) * 8, 8), pl.ds(part * 16, 16), :
                    ].reshape(128, 128)
                    for k in range(2)
                )
                even = jnp.where(low_lanes, first, pltpu.roll(second, 64, 1))
                odd = jnp.where(low_lanes, pltpu.roll(first, 64, 1), second)
                for k, value in enumerate((even, odd)):
                    rows = pl.ds(part * N + k * 128, 128)
                    columns = pl.ds(pair * 128, 128)
                    high, low = split(value)
                    bhigh[rows, columns] = high
                    blow[rows, columns] = low
        both = dot(tz[...], bhigh[...], False)
        partial = both[:512] + both[512:] + dot(tz[:512], blow[...], False)
        for part in range(2):
            high, low = split(partial[part * N : part * N + N])
            whigh[:, pl.ds(part * N, N)] = high
            wlow[:, pl.ds(part * N, N)] = low
        both = dot(ty[...], whigh[...], True)
        field = both[:N] + both[N:] + dot(ty[:N], wlow[...], True)
        obuf[j] = jnp.exp(log_spread * field)
        for step in range(1, 8):
            other = (sa + step) % 8
            pltpu.make_async_remote_copy(
                src_ref=obuf.at[j, pl.ds(pl.multiple_of(other * 32, 32), 32), :],
                dst_ref=out_ref.at[sa, j],
                send_sem=out_send_sem.at[j],
                recv_sem=out_recv_sem.at[j],
                device_id={"sa": other},
                device_id_type=MESH,
            ).start()
        out_ref[sa, j] = obuf[j, pl.ds(pl.multiple_of(sa * 32, 32), 32), :]
        return carry

    lax.fori_loop(0, CHUNKS, finish, 0)

    def drain(j, carry):
        sent = rbuf.at[j, pl.ds(0, GROUP - 1)]
        pltpu.make_async_copy(sent, sent, send_sem.at[j]).wait()
        moved = obuf.at[j, pl.ds(0, 7 * 32), :]
        pltpu.make_async_copy(moved, moved, out_send_sem.at[j]).wait()
        pltpu.make_async_copy(moved, moved, out_recv_sem.at[j]).wait()
        return carry

    lax.fori_loop(0, CHUNKS, drain, 0)


def local(real_coeffs, imaginary_coeffs):
    anywhere = pl.BlockSpec(memory_space=pl.ANY)
    return pl.pallas_call(
        kernel,
        out_shape=jax.ShapeDtypeStruct((8, CHUNKS, 32, N), jnp.float32),
        in_specs=[anywhere] * 5,
        out_specs=pl.BlockSpec(memory_space=pltpu.VMEM),
        scratch_shapes=[
            pltpu.VMEM((4, 64, PITCH, 128), jnp.float32),
            pltpu.VMEM((2048, 512), jnp.bfloat16),
            pltpu.VMEM((2048, 512), jnp.bfloat16),
            pltpu.VMEM((CHUNKS * GROUP * PITCH, 128), jnp.float32),
            pltpu.VMEM((CHUNKS, GROUP, 32, 128), jnp.float32),
            pltpu.VMEM((CHUNKS, N, N), jnp.float32),
            pltpu.VMEM((CHUNKS, 128, 512), jnp.bfloat16),
            pltpu.VMEM((1024, 512), jnp.bfloat16),
            pltpu.VMEM((512, 512), jnp.bfloat16),
            pltpu.VMEM((N, 512), jnp.bfloat16),
            pltpu.VMEM((N, 512), jnp.bfloat16),
            pltpu.VMEM((512, N), jnp.bfloat16),
            pltpu.VMEM((512, N), jnp.bfloat16),
            pltpu.SemaphoreType.DMA((4, 4)),
            pltpu.SemaphoreType.DMA((3,)),
            pltpu.SemaphoreType.DMA((CHUNKS,)),
            pltpu.SemaphoreType.DMA((CHUNKS,)),
            pltpu.SemaphoreType.DMA((CHUNKS,)),
            pltpu.SemaphoreType.DMA((CHUNKS,)),
        ],
        compiler_params=pltpu.CompilerParams(
            collective_id=0, has_side_effects=True, vmem_limit_bytes=56 * 1024 * 1024
        ),
    )(real_coeffs, imaginary_coeffs, x_table(), z_table(), y_table())


def solution(mesh):
    placed = (P("sa", "px", "py", None), P("sa", "px", "py", None))
    return jax.shard_map(
        local,
        mesh=mesh,
        in_specs=placed,
        out_specs=P(None, ("px", "py"), "sa", None),
        check_vma=False,
    )
```

time: 301 us -> 117 us (0.39); the launches traced: 295 us -> 117 us
  waiting for transfers between devices: 137 us -> 0 us
  Pallas kernels: 0 us -> 114 us
  starting transfers between devices: 49.9 us -> 0 us
  matrix products: 40.5 us -> 0 us
  blocking collectives: 37.6 us -> 0 us
  local copies, waits for them, and re-layouts: 30 us -> 3.16 us
    all_to_all x4 -> x0, waiting for transfers between devices: 137 us -> none  [the longest x1 41.9 us: local(): lax.all_to_all(y_imag, ('px', 'py'), split_axis=2, concat_axis=1, tiled=T...]
    pallas_call x0 -> x1, Pallas kernels: none -> 114 us  [local(): pl.pallas_call(kernel, out_shape=jax.ShapeDtypeStruct((8, CHUNKS, 32, N),...]
    all_to_all x4 -> x0, starting transfers between devices: 49.9 us -> none  [the longest x1 26.9 us: local(): lax.all_to_all(y_real, ('px', 'py'), split_axis=2, concat_axis=1, tiled=T...]
    dot_general x10 -> x0, matrix products: 40.5 us -> none  [the longest x4 15.5 us: transform(): real_out = product(cos_table, real_in) - product(sin_table, imag_in)]
    all_to_all x1 -> x0, blocking collectives: 37.6 us -> none  [local(): lax.all_to_all(local_field, 'sa', split_axis=2, concat_axis=0, tiled=True)]
    all_to_all x9 -> x0, local copies, waits for them, and re-layouts: 13.7 us -> none  [the longest x2 4.29 us: local(): lax.all_to_all(x_real, 'px', split_axis=2, concat_axis=1, tiled=True)]
    add x2 -> x0, local copies, waits for them, and re-layouts: 5.09 us -> none  [transform(): imag_out = product(sin_table, real_in) + product(cos_table, imag_in)]
    sub x2 -> x0, local copies, waits for them, and re-layouts: 5.08 us -> none  [transform(): real_out = product(cos_table, real_in) - product(sin_table, imag_in)]
  transfers between devices with their start and end apart: 4 -> 0, of which waited for: 4 -> 0; matrix products, arithmetic and copies ran while one was open for 10% -> 0% of each run, Pallas kernels for 0% -> 0%
where the time goes in v1:
time: 117 us
  Pallas kernels  114 us (97%)
  local copies, waits for them, and re-layouts  3.16 us (3%)
    pallas_call x1, Pallas kernels, local(): pl.pallas_call(kernel, out_shape=jax.ShapeDtypeStruct((8, CHUNKS, 32, N),...  114 us
    unnamed x1, local copies, waits for them, and re-layouts  3.16 us

profile of v1, /device:TPU:1, one launch (start us, length us, event | category | flops | bytes accessed | tf_op | source)
XLA Modules:
  0.0 116.9 jit_solution(4542826202013605971)
XLA Ops:
  0.0 113.8 %shard_map.55 = f32[8,8,32,256]{3,2,1,0:T(8,128)} custom-call(f32[1,64,32,256]{3,2,1,0:T(8,128)} %re_hbm.1, f32[1,64,32,256]{3,2,1,0:T(8,128)} %im_hbm.1, bf16[8,128,512]{2,1,0:T(8,128)(2,1)} %constant.6.clone.tx_hbm, bf16[1024,512]{1,0:T(8,128)(2,1)} %constant.7.clone.tz_hbm, bf16[512,512]{1,0:T(8,128)(2,1)} %constant.8.clone.ty_hbm), custom_call_target="tpu_custom_call" | custom-call | tf_op jit(solution)/shard_map/pallas_call | solution.py:266
  113.8 3.2 %copy.7 = f32[8,8,32,256]{3,2,1,0:T(8,128)} copy(f32[8,8,32,256]{3,2,1,0:T(8,128)} %shard_map.55) | data formatting | bytes 4194304

commit v2 on v1

v2 whole, which is shorter than its diff:
```python
import math

import jax
import jax.numpy as jnp
import numpy as np
from jax import lax
from jax.experimental import pallas as pl
from jax.experimental.pallas import tpu as pltpu
from jax.sharding import PartitionSpec as P

MESH = pl.DeviceIdType.MESH
corr_length = 1.0
log_spread = 0.5

N = 256
GROUP = 32
CHUNKS = 8
PITCH = 40


def matern(squared, length):
    return 1.0 / (1.0 + (2.0 * math.pi * corr_length / length) ** 2 * squared)


def matern_scale(length):
    middle = length // 2
    square_counts = {}
    for position in range(length):
        square_value = ((position + middle) % length - middle) ** 2
        square_counts[square_value] = square_counts.get(square_value, 0) + 1
    plane_counts = {}
    for first_square, first_count in square_counts.items():
        for second_square, second_count in square_counts.items():
            plane_sum = first_square + second_square
            plane_counts[plane_sum] = plane_counts.get(plane_sum, 0) + first_count * second_count
    running = 0.0
    for first_square, first_count in square_counts.items():
        for plane_sum, plane_count in plane_counts.items():
            running = (
                running + first_count * plane_count * matern(first_square + plane_sum, length) ** 2
            )
    return 1.0 / math.sqrt(running)


def halves(table):
    high = table.astype(np.float32).astype(jnp.bfloat16)
    low = (table - high.astype(np.float64)).astype(np.float32).astype(jnp.bfloat16)
    return high, low


def phases(rows, columns):
    angles = (np.asarray(rows)[:, None] * np.asarray(columns)[None, :] % N) * (2.0 * np.pi / N)
    return np.cos(angles), np.sin(angles)


def x_table():
    pieces = []
    for j in range(CHUNKS):
        cos, sin = phases(np.arange(GROUP) * CHUNKS + j, np.arange(N))
        pieces.append(np.block([[cos, -sin], [sin, cos]]))
    high, low = halves(np.stack(pieces))
    return np.concatenate([high, low], axis=1).reshape(-1, 2 * N)


def z_table():
    odd, owner, block, part, row = np.meshgrid(
        *(np.arange(n) for n in (2, 8, 4, 2, 4)), indexing="ij"
    )
    waves = (owner * 32 + (block * 4 + row) * 2 + odd).reshape(-1)
    real = part.reshape(-1)[None, :] == 0
    cos, sin = phases(np.arange(N), waves)
    high, low = halves(np.concatenate([np.where(real, cos, -sin), np.where(real, sin, cos)]))
    return np.concatenate([high, low], axis=0)


def y_table():
    cos, sin = phases(np.arange(N), np.arange(N))
    high, low = halves(np.concatenate([cos, -sin], axis=1))
    return np.concatenate([high, low], axis=0)


def split(value):
    high = value.astype(jnp.bfloat16)
    low = (value - high.astype(jnp.float32)).astype(jnp.bfloat16)
    return high, low


def dot(left, right, transposed):
    return lax.dot_general(
        left,
        right,
        (((1,), (1 if transposed else 0,)), ((), ())),
        preferred_element_type=jnp.float32,
    )


def signed(positions):
    return ((positions + N // 2) % N - N // 2).astype(jnp.float32)


def kernel(
    re_hbm, im_hbm, tables_hbm, out_ref,
    xbuf, dhigh, dlow, gbuf, rbuf, obuf, tx, tz, ty, whigh, wlow, bhigh, blow,
    in_sem, table_sem, send_sem, recv_sem, out_send_sem, out_recv_sem,
):
    px, py, sa = lax.axis_index("px"), lax.axis_index("py"), lax.axis_index("sa")
    me = px * 8 + py
    z, y = px * 2 + lax.div(py, 4), lax.rem(py, 4)

    in_copies = []
    for block in range(4):
        group = []
        for part, source in enumerate((re_hbm, im_hbm)):
            for half in range(2):
                group.append(
                    pltpu.make_async_copy(
                        source.at[0, :, pl.ds(block * 8, 8), pl.ds(half * 128, 128)],
                        xbuf.at[part * 2 + half, :, pl.ds(block * 8, 8), :],
                        in_sem.at[block, part * 2 + half],
                    )
                )
        in_copies.append(group)
    table_copies = [
        pltpu.make_async_copy(
            tables_hbm.at[pl.ds(start, size), :], target.at[pl.ds(at, size), :], table_sem.at[i]
        )
        for i, (start, size, target, at) in enumerate(
            ((0, 128, tx, 0), (128, 896, tx, 128), (1024, 1024, tz, 0), (2048, 512, ty, 0))
        )
    ]
    for copy in in_copies[0]:
        copy.start()
    table_copies[0].start()

    def plane_peer(dz, dy):
        z2, y2 = lax.rem(z + (dz + 8) % 8, 8), lax.rem(y + dy, 4)
        return lax.div(z2, 2), lax.rem(z2, 2) * 4 + y2

    order = (4, 3, -3, 2, -2, 1, -1, 0)
    peers = [plane_peer(dz, dy) for dz in order for dy in range(4) if (dz, dy) != (0, 0)]
    others = [lax.rem(sa + step, 8) for step in range(1, 8)]

    barrier = pltpu.get_barrier_semaphore()
    for p, q in peers:
        pl.semaphore_signal(barrier, inc=1, device_id={"px": p, "py": q}, device_id_type=MESH)
    for other in others:
        pl.semaphore_signal(barrier, inc=1, device_id={"sa": other}, device_id_type=MESH)

    for group in in_copies[1:]:
        for copy in group:
            copy.start()
    for copy in table_copies[1:]:
        copy.start()

    scale = matern_scale(N)
    slope = (2.0 * math.pi * corr_length / N) ** 2
    fy = signed(lax.broadcasted_iota(jnp.int32, (64, 128), 0) + px * 64) ** 2
    lanes = lax.broadcasted_iota(jnp.int32, (64, 128), 1)
    flat = signed(lanes) ** 2 + fy, signed(lanes + 128) ** 2 + fy
    lines = xbuf.reshape(4, 64 * PITCH, 128)

    def weigh(k, carry):
        fz = signed(py * 32 + k) ** 2
        rows = pl.ds(pl.multiple_of(k * 64, 64), 64)
        for half in range(2):
            weight = (1.0 / (1.0 + slope * (flat[half] + fz))) * scale
            for part in range(2):
                value = lines[part * 2 + half, pl.ds(k, 64, stride=PITCH), :] * weight
                high, low = split(value)
                columns = pl.ds(part * N + half * 128, 128)
                dhigh[rows, columns] = high
                dlow[rows, columns] = low
        return carry

    def transform(j, block):
        base = j * (GROUP * PITCH)
        table = pl.multiple_of(j * 128, 128)
        for piece in range(2):
            rows = pl.ds(block * 512 + piece * 256, 256)
            both = dot(tx[pl.ds(table, 128), :], dhigh[rows, :], True)
            result = both[:64] + both[64:] + dot(tx[pl.ds(table, 64), :], dlow[rows, :], True)
            for part in range(2):
                for half in range(2):
                    at = base + block * 8 + part * 4 + piece * 2 + half
                    gbuf[pl.ds(at, GROUP, stride=PITCH), :] = result[
                        part * 32 : part * 32 + 32, half * 128 : half * 128 + 128
                    ]

    def send(j, first, count):
        for p, q in peers:
            row = pl.multiple_of((j * GROUP + p * 8 + q) * PITCH + first, 8)
            pltpu.make_async_remote_copy(
                src_ref=gbuf.at[pl.ds(row, count), :],
                dst_ref=rbuf.at[j, me, pl.ds(first, count), :],
                send_sem=send_sem.at[j],
                recv_sem=recv_sem.at[j],
                device_id={"px": p, "py": q},
                device_id_type=MESH,
            ).start()

    def keep(j):
        rbuf[j, me] = gbuf[pl.ds(pl.multiple_of((j * GROUP + me) * PITCH, 8), 32), :]

    for block in range(4):
        for copy in in_copies[block]:
            copy.wait()
        lax.fori_loop(block * 8, block * 8 + 8, weigh, 0)
        if block == 0:
            table_copies[0].wait()
        transform(0, block)
        if block == 0:
            pl.semaphore_wait(barrier, len(peers) + len(others))
        send(0, block * 8, 8)
    keep(0)
    table_copies[1].wait()

    def forward(j, carry):
        for block in range(4):
            transform(j, block)
        send(j, 0, 32)
        keep(j)
        return carry

    lax.fori_loop(1, CHUNKS, forward, 0)
    table_copies[2].wait()
    table_copies[3].wait()

    low_lanes = lax.broadcasted_iota(jnp.int32, (N, 128), 1) < 64

    def finish(j, carry):
        arrived = rbuf.at[j, pl.ds(0, GROUP - 1)]
        pltpu.make_async_copy(arrived, arrived, recv_sem.at[j]).wait()
        for pair in range(2):
            first, second = (
                rbuf[j, pl.ds((pair * 2 + k) * 8, 8)].reshape(N, 128) for k in range(2)
            )
            even = jnp.where(low_lanes, first, pltpu.roll(second, 64, 1))
            odd = jnp.where(low_lanes, pltpu.roll(first, 64, 1), second)
            for k, value in enumerate((even, odd)):
                rows = pl.ds(k * N, N)
                columns = pl.ds(pair * 128, 128)
                high, low = split(value)
                bhigh[rows, columns] = high
                blow[rows, columns] = low
        both = dot(tz[...], bhigh[...], False)
        partial = both[:512] + both[512:] + dot(tz[:512], blow[...], False)
        for part in range(2):
            high, low = split(partial[part * N : part * N + N])
            whigh[:, pl.ds(part * N, N)] = high
            wlow[:, pl.ds(part * N, N)] = low
        both = dot(ty[...], whigh[...], True)
        field = both[:N] + both[N:] + dot(ty[:N], wlow[...], True)
        obuf[j] = jnp.exp(log_spread * field)
        for other in others:
            pltpu.make_async_remote_copy(
                src_ref=obuf.at[j, pl.ds(pl.multiple_of(other * 32, 32), 32), :],
                dst_ref=out_ref.at[sa, j],
                send_sem=out_send_sem.at[j],
                recv_sem=out_recv_sem.at[j],
                device_id={"sa": other},
                device_id_type=MESH,
            ).start()
        out_ref[sa, j] = obuf[j, pl.ds(pl.multiple_of(sa * 32, 32), 32), :]
        return carry

    lax.fori_loop(0, CHUNKS, finish, 0)

    def drain(j, carry):
        sent = rbuf.at[j, pl.ds(0, GROUP - 1)]
        pltpu.make_async_copy(sent, sent, send_sem.at[j]).wait()
        moved = obuf.at[j, pl.ds(0, 7 * 32), :]
        pltpu.make_async_copy(moved, moved, out_send_sem.at[j]).wait()
        pltpu.make_async_copy(moved, moved, out_recv_sem.at[j]).wait()
        return carry

    lax.fori_loop(0, CHUNKS, drain, 0)


def local(real_coeffs, imaginary_coeffs):
    anywhere = pl.BlockSpec(memory_space=pltpu.HBM)
    return pl.pallas_call(
        kernel,
        out_shape=jax.ShapeDtypeStruct((8, CHUNKS, 32, N), jnp.float32),
        in_specs=[anywhere] * 3,
        out_specs=pl.BlockSpec(memory_space=pltpu.VMEM),
        scratch_shapes=[
            pltpu.VMEM((4, 64, PITCH, 128), jnp.float32),
            pltpu.VMEM((2048, 512), jnp.bfloat16),
            pltpu.VMEM((2048, 512), jnp.bfloat16),
            pltpu.VMEM((CHUNKS * GROUP * PITCH, 128), jnp.float32),
            pltpu.VMEM((CHUNKS, GROUP, 32, 128), jnp.float32),
            pltpu.VMEM((CHUNKS, N, N), jnp.float32),
            pltpu.VMEM((CHUNKS * 128, 512), jnp.bfloat16),
            pltpu.VMEM((1024, 512), jnp.bfloat16),
            pltpu.VMEM((512, 512), jnp.bfloat16),
            pltpu.VMEM((N, 512), jnp.bfloat16),
            pltpu.VMEM((N, 512), jnp.bfloat16),
            pltpu.VMEM((512, N), jnp.bfloat16),
            pltpu.VMEM((512, N), jnp.bfloat16),
            pltpu.SemaphoreType.DMA((4, 4)),
            pltpu.SemaphoreType.DMA((4,)),
            pltpu.SemaphoreType.DMA((CHUNKS,)),
            pltpu.SemaphoreType.DMA((CHUNKS,)),
            pltpu.SemaphoreType.DMA((CHUNKS,)),
            pltpu.SemaphoreType.DMA((CHUNKS,)),
        ],
        compiler_params=pltpu.CompilerParams(
            collective_id=0, has_side_effects=True, vmem_limit_bytes=50 * 1024 * 1024
        ),
    )(real_coeffs, imaginary_coeffs, np.concatenate([x_table(), z_table(), y_table()]))


def solution(mesh):
    placed = (P("sa", "px", "py", None), P("sa", "px", "py", None))
    return jax.shard_map(
        local,
        mesh=mesh,
        in_specs=placed,
        out_specs=P(None, ("px", "py"), "sa", None),
        check_vma=False,
    )
```

time: 117 us -> 112 us (0.957)
  Pallas kernels: 114 us -> 110 us
  local copies, waits for them, and re-layouts: 3.16 us -> 1.32 us
    pallas_call x1, Pallas kernels: 114 us -> 110 us  [local(): pl.pallas_call(kernel, out_shape=jax.ShapeDtypeStruct((8, CHUNKS, 32, N),...]
    unnamed x1, local copies, waits for them, and re-layouts: 3.16 us -> 1.32 us
where the time goes in v2:
time: 112 us
  Pallas kernels  110 us (98%)
  local copies, waits for them, and re-layouts  1.32 us (1%)
    pallas_call x1, Pallas kernels, local(): pl.pallas_call(kernel, out_shape=jax.ShapeDtypeStruct((8, CHUNKS, 32, N),...  110 us

profile of v2, /device:TPU:1, one launch (start us, length us, event | category | flops | bytes accessed | tf_op | source)
XLA Modules:
  0.0 111.6 jit_solution(15624339465779781326)
XLA Ops:
  0.0 110.3 %shard_map.37 = f32[8,8,32,256]{3,2,1,0:T(8,128)S(1)} custom-call(f32[1,64,32,256]{3,2,1,0:T(8,128)} %re_hbm.1, f32[1,64,32,256]{3,2,1,0:T(8,128)} %im_hbm.1, bf16[2560,512]{1,0:T(8,128)(2,1)} %constant.2.clone.tables_hbm), custom_call_target="tpu_custom_call" | custom-call | tf_op jit(solution)/shard_map/pallas_call | solution.py:281
  110.3 1.3 %copy.5 = f32[8,8,32,256]{3,2,1,0:T(8,128)} copy(f32[8,8,32,256]{3,2,1,0:T(8,128)S(1)} %shard_map.37) | data formatting | bytes 4194304

commit v3 on v2

--- a/solution.py
+++ b/solution.py
@@ -101,7 +101,7 @@
 def kernel(
     re_hbm, im_hbm, tables_hbm, out_ref,
     xbuf, dhigh, dlow, gbuf, rbuf, obuf, tx, tz, ty, whigh, wlow, bhigh, blow,
-    in_sem, table_sem, send_sem, recv_sem, out_send_sem, out_recv_sem,
+    in_sem, table_sem, send_sem, recv_sem, out_send_sem, out_recv_sem, ready_sem,
 ):
     px, py, sa = lax.axis_index("px"), lax.axis_index("py"), lax.axis_index("sa")
     me = px * 8 + py
@@ -136,15 +136,31 @@
         z2, y2 = lax.rem(z + (dz + 8) % 8, 8), lax.rem(y + dy, 4)
         return lax.div(z2, 2), lax.rem(z2, 2) * 4 + y2
 
-    order = (4, 3, -3, 2, -2, 1, -1, 0)
-    peers = [plane_peer(dz, dy) for dz in order for dy in range(4) if (dz, dy) != (0, 0)]
-    others = [lax.rem(sa + step, 8) for step in range(1, 8)]
+    near, two, three, four = (
+        [plane_peer(dz, dy) for dz in dzs for dy in range(4) if (dz, dy) != (0, 0)]
+        for dzs in ((1, -1, 0), (2, -2), (3, -3), (4,))
+    )
+    peers = four + three + two + near
+    beside = [plane_peer(1, 0), plane_peer(-1, 0)]
+    x, core = lax.div(sa, 2), lax.rem(sa, 2)
+    others = [
+        lax.rem(x + dx, 4) * 2 + lax.rem(core + dc, 2)
+        for dx in (2, 1, 3, 0)
+        for dc in range(2)
+        if (dx, dc) != (0, 0)
+    ]
 
     barrier = pltpu.get_barrier_semaphore()
-    for p, q in peers:
+    for p, q in near:
         pl.semaphore_signal(barrier, inc=1, device_id={"px": p, "py": q}, device_id_type=MESH)
     for other in others:
         pl.semaphore_signal(barrier, inc=1, device_id={"sa": other}, device_id_type=MESH)
+
+    def tell(level):
+        for p, q in beside:
+            pl.semaphore_signal(
+                ready_sem.at[level], inc=1, device_id={"px": p, "py": q}, device_id_type=MESH
+            )
 
     for group in in_copies[1:]:
         for copy in group:
@@ -186,8 +202,8 @@
                         part * 32 : part * 32 + 32, half * 128 : half * 128 + 128
                     ]
 
-    def send(j, first, count):
-        for p, q in peers:
+    def send(targets, j, first, count):
+        for p, q in targets:
             row = pl.multiple_of((j * GROUP + p * 8 + q) * PITCH + first, 8)
             pltpu.make_async_remote_copy(
                 src_ref=gbuf.at[pl.ds(row, count), :],
@@ -209,15 +225,21 @@
             table_copies[0].wait()
         transform(0, block)
         if block == 0:
-            pl.semaphore_wait(barrier, len(peers) + len(others))
-        send(0, block * 8, 8)
+            pl.semaphore_wait(barrier, len(near) + len(others))
+        else:
+            pl.semaphore_wait(ready_sem.at[block - 1], len(beside))
+        if block < 3:
+            tell(block)
+        send((near, two, three, four)[block], 0, 0, block * 8 + 8)
+        if block > 0:
+            send((near, two + near, three + two + near)[block - 1], 0, block * 8, 8)
     keep(0)
     table_copies[1].wait()
 
     def forward(j, carry):
         for block in range(4):
             transform(j, block)
-        send(j, 0, 32)
+        send(peers, j, 0, 32)
         keep(j)
         return carry
 
@@ -303,6 +325,7 @@
             pltpu.SemaphoreType.DMA((CHUNKS,)),
             pltpu.SemaphoreType.DMA((CHUNKS,)),
             pltpu.SemaphoreType.DMA((CHUNKS,)),
+            pltpu.SemaphoreType.REGULAR((3,)),
         ],
         compiler_params=pltpu.CompilerParams(
             collective_id=0, has_side_effects=True, vmem_limit_bytes=50 * 1024 * 1024

time: 112 us -> 112 us (level)
  no operation moved by 1% of the time
where the time goes in v3:
time: 112 us
  Pallas kernels  110 us (98%)
  local copies, waits for them, and re-layouts  1.32 us (1%)
    pallas_call x1, Pallas kernels, local(): pl.pallas_call(kernel, out_shape=jax.ShapeDtypeStruct((8, CHUNKS, 32, N),...  110 us

profile of v3, /device:TPU:1, one launch (start us, length us, event | category | flops | bytes accessed | tf_op | source)
XLA Modules:
  0.0 111.8 jit_solution(1547672015244692375)
XLA Ops:
  0.0 110.5 %shard_map.37 = f32[8,8,32,256]{3,2,1,0:T(8,128)S(1)} custom-call(f32[1,64,32,256]{3,2,1,0:T(8,128)} %re_hbm.1, f32[1,64,32,256]{3,2,1,0:T(8,128)} %im_hbm.1, bf16[2560,512]{1,0:T(8,128)(2,1)} %constant.2.clone.tables_hbm), custom_call_target="tpu_custom_call" | custom-call | tf_op jit(solution)/shard_map/pallas_call | solution.py:303
  110.5 1.3 %copy.5 = f32[8,8,32,256]{3,2,1,0:T(8,128)} copy(f32[8,8,32,256]{3,2,1,0:T(8,128)S(1)} %shard_map.37) | data formatting | bytes 4194304

commit v4 on v3

--- a/solution.py
+++ b/solution.py
@@ -56,27 +56,25 @@
 def x_table():
     pieces = []
     for j in range(CHUNKS):
-        cos, sin = phases(np.arange(GROUP) * CHUNKS + j, np.arange(N))
-        pieces.append(np.block([[cos, -sin], [sin, cos]]))
-    high, low = halves(np.stack(pieces))
-    return np.concatenate([high, low], axis=1).reshape(-1, 2 * N)
+        cos, sin = phases(np.arange(GROUP) * CHUNKS + j, np.arange(N // 2))
+        pieces += halves(np.block([[cos, -sin], [sin, cos]]))
+    return np.concatenate(pieces, axis=0)
 
 
 def z_table():
-    odd, owner, block, part, row = np.meshgrid(
-        *(np.arange(n) for n in (2, 8, 4, 2, 4)), indexing="ij"
-    )
-    waves = (owner * 32 + (block * 4 + row) * 2 + odd).reshape(-1)
+    owner, block, part, row = np.meshgrid(*(np.arange(n) for n in (8, 4, 2, 4)), indexing="ij")
     real = part.reshape(-1)[None, :] == 0
-    cos, sin = phases(np.arange(N), waves)
-    high, low = halves(np.concatenate([np.where(real, cos, -sin), np.where(real, sin, cos)]))
-    return np.concatenate([high, low], axis=0)
+    pieces = []
+    for odd in range(2):
+        waves = (owner * 32 + (block * 4 + row) * 2 + odd).reshape(-1)
+        cos, sin = phases(np.arange(N // 2), waves)
+        pieces += halves(np.concatenate([np.where(real, cos, -sin), np.where(real, sin, cos)]))
+    return np.concatenate(pieces, axis=0)
 
 
 def y_table():
     cos, sin = phases(np.arange(N), np.arange(N))
-    high, low = halves(np.concatenate([cos, -sin], axis=1))
-    return np.concatenate([high, low], axis=0)
+    return np.concatenate([*halves(cos), *halves(-sin)], axis=0)
 
 
 def split(value):
@@ -100,7 +98,7 @@
 
 def kernel(
     re_hbm, im_hbm, tables_hbm, out_ref,
-    xbuf, dhigh, dlow, gbuf, rbuf, obuf, tx, tz, ty, whigh, wlow, bhigh, blow,
+    wbuf, xbuf, dhigh, dlow, gbuf, rbuf, obuf, tx, tz, ty, whigh, wlow, bhigh, blow,
     in_sem, table_sem, send_sem, recv_sem, out_send_sem, out_recv_sem, ready_sem,
 ):
     px, py, sa = lax.axis_index("px"), lax.axis_index("py"), lax.axis_index("sa")
@@ -125,8 +123,15 @@
             tables_hbm.at[pl.ds(start, size), :], target.at[pl.ds(at, size), :], table_sem.at[i]
         )
         for i, (start, size, target, at) in enumerate(
-            ((0, 128, tx, 0), (128, 896, tx, 128), (1024, 1024, tz, 0), (2048, 512, ty, 0))
+            ((0, 128, tx, 0), (128, 896, tx, 128), (1024, 1024, tz, 0))
         )
+    ] + [
+        pltpu.make_async_copy(
+            tables_hbm.at[pl.ds(2048 + part * 512, 512), :],
+            ty.at[:, pl.ds(part * N, N)],
+            table_sem.at[3 + part],
+        )
+        for part in range(2)
     ]
     for copy in in_copies[0]:
         copy.start()
@@ -136,12 +141,12 @@
         z2, y2 = lax.rem(z + (dz + 8) % 8, 8), lax.rem(y + dy, 4)
         return lax.div(z2, 2), lax.rem(z2, 2) * 4 + y2
 
-    near, two, three, four = (
+    near, far = (
         [plane_peer(dz, dy) for dz in dzs for dy in range(4) if (dz, dy) != (0, 0)]
-        for dzs in ((1, -1, 0), (2, -2), (3, -3), (4,))
+        for dzs in ((2, -2, 1, -1, 0), (4, 3, -3))
     )
-    peers = four + three + two + near
-    beside = [plane_peer(1, 0), plane_peer(-1, 0)]
+    peers = far + near
+    beside = [plane_peer(2, 0), plane_peer(-2, 0)]
     x, core = lax.div(sa, 2), lax.rem(sa, 2)
     others = [
         lax.rem(x + dx, 4) * 2 + lax.rem(core + dc, 2)
@@ -156,12 +161,6 @@
     for other in others:
         pl.semaphore_signal(barrier, inc=1, device_id={"sa": other}, device_id_type=MESH)
 
-    def tell(level):
-        for p, q in beside:
-            pl.semaphore_signal(
-                ready_sem.at[level], inc=1, device_id={"px": p, "py": q}, device_id_type=MESH
-            )
-
     for group in in_copies[1:]:
         for copy in group:
             copy.start()
@@ -175,26 +174,36 @@
     flat = signed(lanes) ** 2 + fy, signed(lanes + 128) ** 2 + fy
     lines = xbuf.reshape(4, 64 * PITCH, 128)
 
-    def weigh(k, carry):
+    def prepare(k, carry):
         fz = signed(py * 32 + k) ** 2
         rows = pl.ds(pl.multiple_of(k * 64, 64), 64)
         for half in range(2):
-            weight = (1.0 / (1.0 + slope * (flat[half] + fz))) * scale
-            for part in range(2):
-                value = lines[part * 2 + half, pl.ds(k, 64, stride=PITCH), :] * weight
+            wbuf[half, rows, :] = (1.0 / (1.0 + slope * (flat[half] + fz))) * scale
+        return carry
+
+    def weigh(k, carry):
+        rows = pl.ds(pl.multiple_of(k * 64, 64), 64)
+        for part in range(2):
+            columns = pl.ds(part * 128, 128)
+            first, second = (
+                lines[part * 2 + half, pl.ds(k, 64, stride=PITCH), :] * wbuf[half, rows, :]
+                for half in range(2)
+            )
+            for odd, value in enumerate((first + second, first - second)):
                 high, low = split(value)
-                columns = pl.ds(part * N + half * 128, 128)
-                dhigh[rows, columns] = high
-                dlow[rows, columns] = low
+                dhigh[odd, rows, columns] = high
+                dlow[odd, rows, columns] = low
         return carry
 
     def transform(j, block):
         base = j * (GROUP * PITCH)
         table = pl.multiple_of(j * 128, 128)
+        odd = j % 2 if isinstance(j, int) else lax.rem(j, 2)
         for piece in range(2):
             rows = pl.ds(block * 512 + piece * 256, 256)
-            both = dot(tx[pl.ds(table, 128), :], dhigh[rows, :], True)
-            result = both[:64] + both[64:] + dot(tx[pl.ds(table, 64), :], dlow[rows, :], True)
+            both = dot(tx[pl.ds(table, 128), :], dhigh[odd, rows, :], True)
+            rest = dot(tx[pl.ds(table, 64), :], dlow[odd, rows, :], True)
+            result = both[:64] + both[64:] + rest
             for part in range(2):
                 for half in range(2):
                     at = base + block * 8 + part * 4 + piece * 2 + half
@@ -217,6 +226,7 @@
     def keep(j):
         rbuf[j, me] = gbuf[pl.ds(pl.multiple_of((j * GROUP + me) * PITCH, 8), 32), :]
 
+    lax.fori_loop(0, 32, prepare, 0)
     for block in range(4):
         for copy in in_copies[block]:
             copy.wait()
@@ -224,15 +234,16 @@
         if block == 0:
             table_copies[0].wait()
         transform(0, block)
-        if block == 0:
+        if block == 1:
             pl.semaphore_wait(barrier, len(near) + len(others))
-        else:
-            pl.semaphore_wait(ready_sem.at[block - 1], len(beside))
-        if block < 3:
-            tell(block)
-        send((near, two, three, four)[block], 0, 0, block * 8 + 8)
-        if block > 0:
-            send((near, two + near, three + two + near)[block - 1], 0, block * 8, 8)
+            for p, q in beside:
+                pl.semaphore_signal(
+                    ready_sem, inc=1, device_id={"px": p, "py": q}, device_id_type=MESH
+                )
+            send(near, 0, 0, 16)
+    pl.semaphore_wait(ready_sem, len(beside))
+    send(far, 0, 0, 32)
+    send(near, 0, 16, 16)
     keep(0)
     table_copies[1].wait()
 
@@ -244,8 +255,8 @@
         return carry
 
     lax.fori_loop(1, CHUNKS, forward, 0)
-    table_copies[2].wait()
-    table_copies[3].wait()
+    for copy in table_copies[2:]:
+        copy.wait()
 
     low_lanes = lax.broadcasted_iota(jnp.int32, (N, 128), 1) < 64
 
@@ -264,12 +275,18 @@
                 high, low = split(value)
                 bhigh[rows, columns] = high
                 blow[rows, columns] = low
-        both = dot(tz[...], bhigh[...], False)
-        partial = both[:512] + both[512:] + dot(tz[:512], blow[...], False)
-        for part in range(2):
-            high, low = split(partial[part * N : part * N + N])
-            whigh[:, pl.ds(part * N, N)] = high
-            wlow[:, pl.ds(part * N, N)] = low
+        terms = []
+        for odd in range(2):
+            rows, above = pl.ds(odd * N, N), odd * 512
+            both = dot(tz[above : above + 512], bhigh[rows, :], False)
+            rest = dot(tz[above : above + N], blow[rows, :], False)
+            terms.append(both[:N] + both[N:] + rest)
+        for upper, value in enumerate((terms[0] + terms[1], terms[0] - terms[1])):
+            rows = pl.ds(upper * 128, 128)
+            for part in range(2):
+                high, low = split(value[part * 128 : part * 128 + 128])
+                whigh[rows, pl.ds(part * N, N)] = high
+                wlow[rows, pl.ds(part * N, N)] = low
         both = dot(ty[...], whigh[...], True)
         field = both[:N] + both[N:] + dot(ty[:N], wlow[...], True)
         obuf[j] = jnp.exp(log_spread * field)
@@ -300,37 +317,40 @@
 
 def local(real_coeffs, imaginary_coeffs):
     anywhere = pl.BlockSpec(memory_space=pltpu.HBM)
+    spare = np.zeros((2048, N), jnp.bfloat16)
+    tables = np.concatenate([x_table(), z_table(), y_table(), spare])
     return pl.pallas_call(
         kernel,
         out_shape=jax.ShapeDtypeStruct((8, CHUNKS, 32, N), jnp.float32),
         in_specs=[anywhere] * 3,
         out_specs=pl.BlockSpec(memory_space=pltpu.VMEM),
         scratch_shapes=[
+            pltpu.VMEM((2, 2048, 128), jnp.float32),
             pltpu.VMEM((4, 64, PITCH, 128), jnp.float32),
-            pltpu.VMEM((2048, 512), jnp.bfloat16),
-            pltpu.VMEM((2048, 512), jnp.bfloat16),
+            pltpu.VMEM((2, 2048, N), jnp.bfloat16),
+            pltpu.VMEM((2, 2048, N), jnp.bfloat16),
             pltpu.VMEM((CHUNKS * GROUP * PITCH, 128), jnp.float32),
             pltpu.VMEM((CHUNKS, GROUP, 32, 128), jnp.float32),
             pltpu.VMEM((CHUNKS, N, N), jnp.float32),
-            pltpu.VMEM((CHUNKS * 128, 512), jnp.bfloat16),
-            pltpu.VMEM((1024, 512), jnp.bfloat16),
+            pltpu.VMEM((CHUNKS * 128, N), jnp.bfloat16),
+            pltpu.VMEM((1024, N), jnp.bfloat16),
             pltpu.VMEM((512, 512), jnp.bfloat16),
             pltpu.VMEM((N, 512), jnp.bfloat16),
             pltpu.VMEM((N, 512), jnp.bfloat16),
             pltpu.VMEM((512, N), jnp.bfloat16),
             pltpu.VMEM((512, N), jnp.bfloat16),
             pltpu.SemaphoreType.DMA((4, 4)),
-            pltpu.SemaphoreType.DMA((4,)),
+            pltpu.SemaphoreType.DMA((5,)),
             pltpu.SemaphoreType.DMA((CHUNKS,)),
             pltpu.SemaphoreType.DMA((CHUNKS,)),
             pltpu.SemaphoreType.DMA((CHUNKS,)),
             pltpu.SemaphoreType.DMA((CHUNKS,)),
-            pltpu.SemaphoreType.REGULAR((3,)),
+            pltpu.SemaphoreType.REGULAR,
         ],
         compiler_params=pltpu.CompilerParams(
             collective_id=0, has_side_effects=True, vmem_limit_bytes=50 * 1024 * 1024
         ),
-    )(real_coeffs, imaginary_coeffs, np.concatenate([x_table(), z_table(), y_table()]))
+    )(real_coeffs, imaginary_coeffs, tables)
 
 
 def solution(mesh):

time: 112 us -> 111 us (level)
  no operation moved by 1% of the time
where the time goes in v4:
time: 111 us
  Pallas kernels  110 us (99%)
  local copies, waits for them, and re-layouts  1.32 us (1%)
    pallas_call x1, Pallas kernels, local(): pl.pallas_call(kernel, out_shape=jax.ShapeDtypeStruct((8, CHUNKS, 32, N),...  110 us

profile of v4, /device:TPU:1, one launch (start us, length us, event | category | flops | bytes accessed | tf_op | source)
XLA Modules:
  0.0 110.9 jit_solution(9308363931707394106)
XLA Ops:
  0.0 109.6 %shard_map.37 = f32[8,8,32,256]{3,2,1,0:T(8,128)S(1)} custom-call(f32[1,64,32,256]{3,2,1,0:T(8,128)} %re_hbm.1, f32[1,64,32,256]{3,2,1,0:T(8,128)} %im_hbm.1, bf16[5120,256]{1,0:T(8,128)(2,1)} %constant.2.clone.tables_hbm), custom_call_target="tpu_custom_call" | custom-call | tf_op jit(solution)/shard_map/pallas_call | solution.py:322
  109.6 1.3 %copy.5 = f32[8,8,32,256]{3,2,1,0:T(8,128)} copy(f32[8,8,32,256]{3,2,1,0:T(8,128)S(1)} %shard_map.37) | data formatting | bytes 4194304

commit v5 on v4

--- a/solution.py
+++ b/solution.py
@@ -98,8 +98,8 @@
 
 def kernel(
     re_hbm, im_hbm, tables_hbm, out_ref,
-    wbuf, xbuf, dhigh, dlow, gbuf, rbuf, obuf, tx, tz, ty, whigh, wlow, bhigh, blow,
-    in_sem, table_sem, send_sem, recv_sem, out_send_sem, out_recv_sem, ready_sem,
+    wbuf, xbuf, dhigh, dlow, gbuf, hbuf, rbuf, obuf, tx, tz, ty, whigh, wlow, bhigh, blow,
+    in_sem, table_sem, send_sem, recv_sem, out_send_sem, out_recv_sem, mate_sem, ready_sem,
 ):
     px, py, sa = lax.axis_index("px"), lax.axis_index("py"), lax.axis_index("sa")
     me = px * 8 + py
@@ -148,6 +148,12 @@
     peers = far + near
     beside = [plane_peer(2, 0), plane_peer(-2, 0)]
     x, core = lax.div(sa, 2), lax.rem(sa, 2)
+    mate = x * 2 + (1 - core)
+    places = [(dz, dy) for dz in (4, 3, -3, 2, -2, 1, -1, 0) for dy in (1, 0)]
+
+    def shared(of_core):
+        return [plane_peer(dz, of_core * 2 + dy) for dz, dy in places]
+
     others = [
         lax.rem(x + dx, 4) * 2 + lax.rem(core + dc, 2)
         for dx in (2, 1, 3, 0)
@@ -247,6 +253,24 @@
     keep(0)
     table_copies[1].wait()
 
+    last = CHUNKS - 1
+
+    def message(p, q):
+        return gbuf.at[pl.ds(pl.multiple_of((last * GROUP + p * 8 + q) * PITCH, 8), 32), :]
+
+    for block in range(4):
+        transform(last, block)
+    keep(last)
+    for slot, (p, q) in enumerate(shared(1 - core)):
+        pltpu.make_async_remote_copy(
+            src_ref=message(p, q),
+            dst_ref=hbuf.at[slot],
+            send_sem=mate_sem.at[0],
+            recv_sem=mate_sem.at[1],
+            device_id={"sa": mate},
+            device_id_type=MESH,
+        ).start()
+
     def forward(j, carry):
         for block in range(4):
             transform(j, block)
@@ -254,7 +278,35 @@
         keep(j)
         return carry
 
-    lax.fori_loop(1, CHUNKS, forward, 0)
+    lax.fori_loop(1, last, forward, 0)
+    pltpu.make_async_copy(hbuf, hbuf, mate_sem.at[1]).wait()
+
+    def send_last(own):
+        def one(slot, p, q):
+            pltpu.make_async_remote_copy(
+                src_ref=message(p, q) if own else hbuf.at[slot],
+                dst_ref=rbuf.at[last, me],
+                send_sem=send_sem.at[last],
+                recv_sem=recv_sem.at[last],
+                device_id={"px": p, "py": q, "sa": sa if own else mate},
+                device_id_type=MESH,
+            ).start()
+
+        *most, final = shared(core)
+        for slot, (p, q) in enumerate(most):
+            one(slot, p, q)
+        pl.when(core == 1)(lambda: one(len(most), *final))
+
+    @pl.when(core == 0)
+    def _():
+        send_last(True)
+        send_last(False)
+
+    @pl.when(core == 1)
+    def _():
+        send_last(False)
+        send_last(True)
+
     for copy in table_copies[2:]:
         copy.wait()
 
@@ -304,9 +356,19 @@
 
     lax.fori_loop(0, CHUNKS, finish, 0)
 
-    def drain(j, carry):
+    for served in range(2):
+        sent = rbuf.at[last, pl.ds(0, 30 + 2 * served)]
+        pl.when(core == served)(pltpu.make_async_copy(sent, sent, send_sem.at[last]).wait)
+    pltpu.make_async_copy(hbuf, hbuf, mate_sem.at[0]).wait()
+
+    def drain_sent(j, carry):
         sent = rbuf.at[j, pl.ds(0, GROUP - 1)]
         pltpu.make_async_copy(sent, sent, send_sem.at[j]).wait()
+        return carry
+
+    lax.fori_loop(0, last, drain_sent, 0)
+
+    def drain(j, carry):
         moved = obuf.at[j, pl.ds(0, 7 * 32), :]
         pltpu.make_async_copy(moved, moved, out_send_sem.at[j]).wait()
         pltpu.make_async_copy(moved, moved, out_recv_sem.at[j]).wait()
@@ -330,6 +392,7 @@
             pltpu.VMEM((2, 2048, N), jnp.bfloat16),
             pltpu.VMEM((2, 2048, N), jnp.bfloat16),
             pltpu.VMEM((CHUNKS * GROUP * PITCH, 128), jnp.float32),
+            pltpu.VMEM((GROUP // 2, 32, 128), jnp.float32),
             pltpu.VMEM((CHUNKS, GROUP, 32, 128), jnp.float32),
             pltpu.VMEM((CHUNKS, N, N), jnp.float32),
             pltpu.VMEM((CHUNKS * 128, N), jnp.bfloat16),
@@ -345,6 +408,7 @@
             pltpu.SemaphoreType.DMA((CHUNKS,)),
             pltpu.SemaphoreType.DMA((CHUNKS,)),
             pltpu.SemaphoreType.DMA((CHUNKS,)),
+            pltpu.SemaphoreType.DMA((2,)),
             pltpu.SemaphoreType.REGULAR,
         ],
         compiler_params=pltpu.CompilerParams(

time: 111 us -> 109 us (0.982)
  Pallas kernels: 110 us -> 108 us
    pallas_call x1, Pallas kernels: 110 us -> 108 us  [local(): pl.pallas_call(kernel, out_shape=jax.ShapeDtypeStruct((8, CHUNKS, 32, N),...]
where the time goes in v5:
time: 109 us
  Pallas kernels  108 us (99%)
  local copies, waits for them, and re-layouts  1.32 us (1%)
    pallas_call x1, Pallas kernels, local(): pl.pallas_call(kernel, out_shape=jax.ShapeDtypeStruct((8, CHUNKS, 32, N),...  108 us

profile of v5, /device:TPU:1, one launch (start us, length us, event | category | flops | bytes accessed | tf_op | source)
XLA Modules:
  0.0 109.1 jit_solution(612410434644697483)
XLA Ops:
  0.0 107.8 %shard_map.37 = f32[8,8,32,256]{3,2,1,0:T(8,128)S(1)} custom-call(f32[1,64,32,256]{3,2,1,0:T(8,128)} %re_hbm.1, f32[1,64,32,256]{3,2,1,0:T(8,128)} %im_hbm.1, bf16[5120,256]{1,0:T(8,128)(2,1)} %constant.2.clone.tables_hbm), custom_call_target="tpu_custom_call" | custom-call | tf_op jit(solution)/shard_map/pallas_call | solution.py:384
  107.8 1.3 %copy.5 = f32[8,8,32,256]{3,2,1,0:T(8,128)} copy(f32[8,8,32,256]{3,2,1,0:T(8,128)S(1)} %shard_map.37) | data formatting | bytes 4194304

commit v6 on v5

--- a/solution.py
+++ b/solution.py
@@ -125,13 +125,6 @@
         for i, (start, size, target, at) in enumerate(
             ((0, 128, tx, 0), (128, 896, tx, 128), (1024, 1024, tz, 0))
         )
-    ] + [
-        pltpu.make_async_copy(
-            tables_hbm.at[pl.ds(2048 + part * 512, 512), :],
-            ty.at[:, pl.ds(part * N, N)],
-            table_sem.at[3 + part],
-        )
-        for part in range(2)
     ]
     for copy in in_copies[0]:
         copy.start()
@@ -156,9 +149,7 @@
 
     others = [
         lax.rem(x + dx, 4) * 2 + lax.rem(core + dc, 2)
-        for dx in (2, 1, 3, 0)
-        for dc in range(2)
-        if (dx, dc) != (0, 0)
+        for dx, dc in ((2, 1), (2, 0), (1, 1), (3, 1), (1, 0), (3, 0), (0, 1))
     ]
 
     barrier = pltpu.get_barrier_semaphore()
@@ -172,7 +163,6 @@
             copy.start()
     for copy in table_copies[1:]:
         copy.start()
-
     scale = matern_scale(N)
     slope = (2.0 * math.pi * corr_length / N) ** 2
     fy = signed(lax.broadcasted_iota(jnp.int32, (64, 128), 0) + px * 64) ** 2
@@ -240,17 +230,31 @@
         if block == 0:
             table_copies[0].wait()
         transform(0, block)
-        if block == 1:
+        if block == 0:
             pl.semaphore_wait(barrier, len(near) + len(others))
             for p, q in beside:
                 pl.semaphore_signal(
                     ready_sem, inc=1, device_id={"px": p, "py": q}, device_id_type=MESH
                 )
-            send(near, 0, 0, 16)
+        if block < 3:
+            send(near, 0, block * 8, 8)
     pl.semaphore_wait(ready_sem, len(beside))
     send(far, 0, 0, 32)
-    send(near, 0, 16, 16)
+    send(near, 0, 24, 8)
     keep(0)
+
+    for part in range(2):
+        for precision in range(2):
+            for place, owner in enumerate([*others, sa]):
+                half, slot = divmod(place, 4)
+                pltpu.make_async_copy(
+                    tables_hbm.at[
+                        pl.ds(pl.multiple_of(2048 + part * 512 + precision * N + owner * 32, 32), 32), :
+                    ],
+                    ty.at[pl.ds(half * N + precision * 128 + slot * 32, 32), pl.ds(part * N, N)],
+                    table_sem.at[3],
+                ).start()
+
     table_copies[1].wait()
 
     last = CHUNKS - 1
@@ -307,8 +311,8 @@
         send_last(False)
         send_last(True)
 
-    for copy in table_copies[2:]:
-        copy.wait()
+    table_copies[2].wait()
+    pltpu.make_async_copy(ty, ty, table_sem.at[3]).wait()
 
     low_lanes = lax.broadcasted_iota(jnp.int32, (N, 128), 1) < 64
 
@@ -330,28 +334,34 @@
         terms = []
         for odd in range(2):
             rows, above = pl.ds(odd * N, N), odd * 512
-            both = dot(tz[above : above + 512], bhigh[rows, :], False)
-            rest = dot(tz[above : above + N], blow[rows, :], False)
-            terms.append(both[:N] + both[N:] + rest)
+            high, low = tz[above : above + N], tz[above + N : above + 2 * N]
+            terms.append(
+                dot(high, bhigh[rows, :], False)
+                + dot(low, bhigh[rows, :], False)
+                + dot(high, blow[rows, :], False)
+            )
         for upper, value in enumerate((terms[0] + terms[1], terms[0] - terms[1])):
             rows = pl.ds(upper * 128, 128)
             for part in range(2):
                 high, low = split(value[part * 128 : part * 128 + 128])
                 whigh[rows, pl.ds(part * N, N)] = high
                 wlow[rows, pl.ds(part * N, N)] = low
-        both = dot(ty[...], whigh[...], True)
-        field = both[:N] + both[N:] + dot(ty[:N], wlow[...], True)
-        obuf[j] = jnp.exp(log_spread * field)
-        for other in others:
-            pltpu.make_async_remote_copy(
-                src_ref=obuf.at[j, pl.ds(pl.multiple_of(other * 32, 32), 32), :],
-                dst_ref=out_ref.at[sa, j],
-                send_sem=out_send_sem.at[j],
-                recv_sem=out_recv_sem.at[j],
-                device_id={"sa": other},
-                device_id_type=MESH,
-            ).start()
-        out_ref[sa, j] = obuf[j, pl.ds(pl.multiple_of(sa * 32, 32), 32), :]
+        for half in range(2):
+            both = dot(ty[half * N : half * N + N], whigh[...], True)
+            field = both[:128] + both[128:] + dot(ty[half * N : half * N + 128], wlow[...], True)
+            obuf[j, pl.ds(half * 128, 128), :] = jnp.exp(log_spread * field)
+            for place, other in enumerate(others):
+                if place // 4 != half:
+                    continue
+                pltpu.make_async_remote_copy(
+                    src_ref=obuf.at[j, pl.ds(place * 32, 32), :],
+                    dst_ref=out_ref.at[sa, j],
+                    send_sem=out_send_sem.at[j],
+                    recv_sem=out_recv_sem.at[j],
+                    device_id={"sa": other},
+                    device_id_type=MESH,
+                ).start()
+        out_ref[sa, j] = obuf[j, pl.ds(7 * 32, 32), :]
         return carry
 
     lax.fori_loop(0, CHUNKS, finish, 0)
@@ -403,7 +413,7 @@
             pltpu.VMEM((512, N), jnp.bfloat16),
             pltpu.VMEM((512, N), jnp.bfloat16),
             pltpu.SemaphoreType.DMA((4, 4)),
-            pltpu.SemaphoreType.DMA((5,)),
+            pltpu.SemaphoreType.DMA((4,)),
             pltpu.SemaphoreType.DMA((CHUNKS,)),
             pltpu.SemaphoreType.DMA((CHUNKS,)),
             pltpu.SemaphoreType.DMA((CHUNKS,)),

time: 109 us -> 109 us (level)
  no operation moved by 1% of the time
where the time goes in v6:
time: 109 us
  Pallas kernels  108 us (99%)
  local copies, waits for them, and re-layouts  1.32 us (1%)
    pallas_call x1, Pallas kernels, local(): pl.pallas_call(kernel, out_shape=jax.ShapeDtypeStruct((8, CHUNKS, 32, N),...  108 us

profile of v6, /device:TPU:1, one launch (start us, length us, event | category | flops | bytes accessed | tf_op | source)
XLA Modules:
  0.0 109.4 jit_solution(18324545604927678708)
XLA Ops:
  0.0 108.1 %shard_map.37 = f32[8,8,32,256]{3,2,1,0:T(8,128)S(1)} custom-call(f32[1,64,32,256]{3,2,1,0:T(8,128)} %re_hbm.1, f32[1,64,32,256]{3,2,1,0:T(8,128)} %im_hbm.1, bf16[5120,256]{1,0:T(8,128)(2,1)} %constant.2.clone.tables_hbm), custom_call_target="tpu_custom_call" | custom-call | tf_op jit(solution)/shard_map/pallas_call | solution.py:394
  108.1 1.3 %copy.5 = f32[8,8,32,256]{3,2,1,0:T(8,128)} copy(f32[8,8,32,256]{3,2,1,0:T(8,128)S(1)} %shard_map.37) | data formatting | bytes 4194304

commit v7 on v6

--- a/solution.py
+++ b/solution.py
@@ -149,7 +149,7 @@
 
     others = [
         lax.rem(x + dx, 4) * 2 + lax.rem(core + dc, 2)
-        for dx, dc in ((2, 1), (2, 0), (1, 1), (3, 1), (1, 0), (3, 0), (0, 1))
+        for dx, dc in ((2, 0), (2, 1), (1, 0), (3, 0), (1, 1), (3, 1), (0, 1))
     ]
 
     barrier = pltpu.get_barrier_semaphore()
@@ -163,6 +163,18 @@
             copy.start()
     for copy in table_copies[1:]:
         copy.start()
+    for part in range(2):
+        for precision in range(2):
+            for place, owner in enumerate([*others, sa]):
+                half, slot = divmod(place, 4)
+                pltpu.make_async_copy(
+                    tables_hbm.at[
+                        pl.ds(pl.multiple_of(2048 + part * 512 + precision * N + owner * 32, 32), 32), :
+                    ],
+                    ty.at[pl.ds(half * N + precision * 128 + slot * 32, 32), pl.ds(part * N, N)],
+                    table_sem.at[3],
+                ).start()
+
     scale = matern_scale(N)
     slope = (2.0 * math.pi * corr_length / N) ** 2
     fy = signed(lax.broadcasted_iota(jnp.int32, (64, 128), 0) + px * 64) ** 2
@@ -242,19 +254,6 @@
     send(far, 0, 0, 32)
     send(near, 0, 24, 8)
     keep(0)
-
-    for part in range(2):
-        for precision in range(2):
-            for place, owner in enumerate([*others, sa]):
-                half, slot = divmod(place, 4)
-                pltpu.make_async_copy(
-                    tables_hbm.at[
-                        pl.ds(pl.multiple_of(2048 + part * 512 + precision * N + owner * 32, 32), 32), :
-                    ],
-                    ty.at[pl.ds(half * N + precision * 128 + slot * 32, 32), pl.ds(part * N, N)],
-                    table_sem.at[3],
-                ).start()
-
     table_copies[1].wait()
 
     last = CHUNKS - 1

time: 109 us -> 109 us (level)
  no operation moved by 1% of the time
where the time goes in v7:
time: 109 us
  Pallas kernels  107 us (98%)
  local copies, waits for them, and re-layouts  1.32 us (1%)
    pallas_call x1, Pallas kernels, local(): pl.pallas_call(kernel, out_shape=jax.ShapeDtypeStruct((8, CHUNKS, 32, N),...  107 us

profile of v7, /device:TPU:1, one launch (start us, length us, event | category | flops | bytes accessed | tf_op | source)
XLA Modules:
  0.0 108.7 jit_solution(10677035703478080286)
XLA Ops:
  0.0 107.4 %shard_map.37 = f32[8,8,32,256]{3,2,1,0:T(8,128)S(1)} custom-call(f32[1,64,32,256]{3,2,1,0:T(8,128)} %re_hbm.1, f32[1,64,32,256]{3,2,1,0:T(8,128)} %im_hbm.1, bf16[5120,256]{1,0:T(8,128)(2,1)} %constant.2.clone.tables_hbm), custom_call_target="tpu_custom_call" | custom-call | tf_op jit(solution)/shard_map/pallas_call | solution.py:393
  107.4 1.3 %copy.5 = f32[8,8,32,256]{3,2,1,0:T(8,128)} copy(f32[8,8,32,256]{3,2,1,0:T(8,128)S(1)} %shard_map.37) | data formatting | bytes 4194304

commit v8 on v7

--- a/solution.py
+++ b/solution.py
@@ -149,7 +149,7 @@
 
     others = [
         lax.rem(x + dx, 4) * 2 + lax.rem(core + dc, 2)
-        for dx, dc in ((2, 0), (2, 1), (1, 0), (3, 0), (1, 1), (3, 1), (0, 1))
+        for dx, dc in ((2, 0), (1, 0), (3, 0), (2, 1), (1, 1), (3, 1), (0, 1))
     ]
 
     barrier = pltpu.get_barrier_semaphore()
@@ -163,18 +163,6 @@
             copy.start()
     for copy in table_copies[1:]:
         copy.start()
-    for part in range(2):
-        for precision in range(2):
-            for place, owner in enumerate([*others, sa]):
-                half, slot = divmod(place, 4)
-                pltpu.make_async_copy(
-                    tables_hbm.at[
-                        pl.ds(pl.multiple_of(2048 + part * 512 + precision * N + owner * 32, 32), 32), :
-                    ],
-                    ty.at[pl.ds(half * N + precision * 128 + slot * 32, 32), pl.ds(part * N, N)],
-                    table_sem.at[3],
-                ).start()
-
     scale = matern_scale(N)
     slope = (2.0 * math.pi * corr_length / N) ** 2
     fy = signed(lax.broadcasted_iota(jnp.int32, (64, 128), 0) + px * 64) ** 2
@@ -250,6 +238,18 @@
                 )
         if block < 3:
             send(near, 0, block * 8, 8)
+        if block == 0:
+            for part in range(2):
+                for precision in range(2):
+                    for place, owner in enumerate([*others, sa]):
+                        half, slot = divmod(place, 4)
+                        pltpu.make_async_copy(
+                            tables_hbm.at[
+                                pl.ds(pl.multiple_of(2048 + part * 512 + precision * N + owner * 32, 32), 32), :
+                            ],
+                            ty.at[pl.ds(half * N + precision * 128 + slot * 32, 32), pl.ds(part * N, N)],
+                            table_sem.at[3],
+                        ).start()
     pl.semaphore_wait(ready_sem, len(beside))
     send(far, 0, 0, 32)
     send(near, 0, 24, 8)

time: 109 us -> 109 us (level)
  no operation moved by 1% of the time
where the time goes in v8:
time: 109 us
  Pallas kernels  107 us (98%)
  local copies, waits for them, and re-layouts  1.32 us (1%)
    pallas_call x1, Pallas kernels, local(): pl.pallas_call(kernel, out_shape=jax.ShapeDtypeStruct((8, CHUNKS, 32, N),...  107 us

profile of v8, /device:TPU:1, one launch (start us, length us, event | category | flops | bytes accessed | tf_op | source)
XLA Modules:
  0.0 108.7 jit_solution(7611343348453802971)
XLA Ops:
  0.0 107.4 %shard_map.37 = f32[8,8,32,256]{3,2,1,0:T(8,128)S(1)} custom-call(f32[1,64,32,256]{3,2,1,0:T(8,128)} %re_hbm.1, f32[1,64,32,256]{3,2,1,0:T(8,128)} %im_hbm.1, bf16[5120,256]{1,0:T(8,128)(2,1)} %constant.2.clone.tables_hbm), custom_call_target="tpu_custom_call" | custom-call | tf_op jit(solution)/shard_map/pallas_call | solution.py:393
  107.4 1.3 %copy.5 = f32[8,8,32,256]{3,2,1,0:T(8,128)} copy(f32[8,8,32,256]{3,2,1,0:T(8,128)S(1)} %shard_map.37) | data formatting | bytes 4194304

commit v9 on v8

--- a/solution.py
+++ b/solution.py
@@ -236,8 +236,7 @@
                 pl.semaphore_signal(
                     ready_sem, inc=1, device_id={"px": p, "py": q}, device_id_type=MESH
                 )
-        if block < 3:
-            send(near, 0, block * 8, 8)
+        send(near, 0, block * 8, 8)
         if block == 0:
             for part in range(2):
                 for precision in range(2):
@@ -252,7 +251,6 @@
                         ).start()
     pl.semaphore_wait(ready_sem, len(beside))
     send(far, 0, 0, 32)
-    send(near, 0, 24, 8)
     keep(0)
     table_copies[1].wait()
 

time: 109 us -> 109 us (level)
  no operation moved by 1% of the time
where the time goes in v9:
time: 109 us
  Pallas kernels  107 us (98%)
  local copies, waits for them, and re-layouts  1.32 us (1%)
    pallas_call x1, Pallas kernels, local(): pl.pallas_call(kernel, out_shape=jax.ShapeDtypeStruct((8, CHUNKS, 32, N),...  107 us

profile of v9, /device:TPU:1, one launch (start us, length us, event | category | flops | bytes accessed | tf_op | source)
XLA Modules:
  0.0 108.7 jit_solution(5124234980060825154)
XLA Ops:
  0.0 107.4 %shard_map.37 = f32[8,8,32,256]{3,2,1,0:T(8,128)S(1)} custom-call(f32[1,64,32,256]{3,2,1,0:T(8,128)} %re_hbm.1, f32[1,64,32,256]{3,2,1,0:T(8,128)} %im_hbm.1, bf16[5120,256]{1,0:T(8,128)(2,1)} %constant.2.clone.tables_hbm), custom_call_target="tpu_custom_call" | custom-call | tf_op jit(solution)/shard_map/pallas_call | solution.py:391
  107.4 1.3 %copy.5 = f32[8,8,32,256]{3,2,1,0:T(8,128)} copy(f32[8,8,32,256]{3,2,1,0:T(8,128)S(1)} %shard_map.37) | data formatting | bytes 4194304
